TPU v7x, 32 devices: a whole 2x2x4 slice. The times are simulated.
32 devices in a mesh: cp: 32 (over z, y, x, core).
Axes of the slice: x: 2, y: 2, z: 4, core: 2. Of those that a mesh axis runs over, the one named last changes fastest.
Arguments:
- queries: bfloat16 [4096, 16, 192], P('cp')
- latent: bfloat16 [4096, 512], P('cp')
- key_rope: bfloat16 [4096, 64], P('cp')
- w_uk: bfloat16 [512, 16, 128], replicated
- w_uv: bfloat16 [512, 16, 128], replicated
- d_out: bfloat16 [4096, 16, 128], P('cp')
Outputs:
- output 1: bfloat16 [4096, 16, 128], P('cp')
- output 2: bfloat16 [4096, 16, 192], P('cp')
- output 3: bfloat16 [4096, 512], P('cp')
- output 4: bfloat16 [4096, 64], P('cp')
- output 5: float32 [512, 16, 128], replicated
- output 6: float32 [512, 16, 128], replicated
All inputs are finite; a program needn't handle non-finite values.
Results may differ from a plain program's by a relative error of at most 0.02.
Values are sent between devices in bfloat16 or wider.
A program may use at most 1 GiB of HBM per device.

v0:
```python
import math
import jax
import jax.numpy as jnp
from jax import lax
from jax.sharding import PartitionSpec as P


def solution(mesh):
    n_dev = mesh.shape["cp"]
    seq_spec = P("cp")

    def gather_all(k_nope, values, key_rope):
        k_all = lax.all_gather(k_nope, "cp", tiled=True)
        v_all = lax.all_gather(values, "cp", tiled=True)
        r_all = lax.all_gather(key_rope, "cp", tiled=True)
        return k_all, v_all, r_all

    def local_step(queries, latent, key_rope, w_uk, w_uv, d_out):
        tok_count = queries.shape[0]
        nope_dim = w_uk.shape[-1]
        score_scale = 1.0 / math.sqrt(queries.shape[-1])
        dev_index = lax.axis_index("cp")
        q_nope = queries[:, :, :nope_dim]
        q_rope = queries[:, :, nope_dim:]
        q_pos = dev_index * tok_count + jnp.arange(tok_count)
        visible = jnp.arange(tok_count * n_dev)[None, :] <= q_pos[:, None]

        def masked_scores(k_all, r_all):
            scores = (jnp.einsum("qhd,khd->hqk", q_nope, k_all, preferred_element_type=jnp.float32)
                      + jnp.einsum("qhd,kd->hqk", q_rope, r_all, preferred_element_type=jnp.float32)) * score_scale
            return jnp.where(visible[None], scores, -1e30)

        k_nope = jnp.einsum("tl,lhd->thd", latent, w_uk, preferred_element_type=jnp.float32).astype(jnp.bfloat16)
        values = jnp.einsum("tl,lhd->thd", latent, w_uv, preferred_element_type=jnp.float32).astype(jnp.bfloat16)

        k_all, v_all, r_all = gather_all(k_nope, values, key_rope)
        scores = masked_scores(k_all, r_all)
        row_max = jnp.max(scores, axis=-1, keepdims=True)
        exp_scores = jnp.exp(scores - row_max)
        row_sum = jnp.sum(exp_scores, axis=-1, keepdims=True)
        log_norm = row_max + jnp.log(row_sum)
        fwd_prob = (exp_scores / row_sum).astype(jnp.bfloat16)
        attn_out = jnp.einsum("hqk,khd->qhd", fwd_prob, v_all, preferred_element_type=jnp.float32).astype(jnp.bfloat16)

        k_all, v_all, r_all = gather_all(k_nope, values, key_rope)
        attn_prob = jnp.exp(masked_scores(k_all, r_all) - log_norm)
        prob_b = attn_prob.astype(jnp.bfloat16)
        d_prob = jnp.einsum("qhd,khd->hqk", d_out, v_all, preferred_element_type=jnp.float32)
        row_delta = jnp.einsum("qhd,qhd->hq", d_out, attn_out, preferred_element_type=jnp.float32)[:, :, None]
        d_score = (attn_prob * (d_prob - row_delta) * score_scale).astype(jnp.bfloat16)
        d_q_nope = jnp.einsum("hqk,khd->qhd", d_score, k_all, preferred_element_type=jnp.float32)
        d_q_rope = jnp.einsum("hqk,kd->qhd", d_score, r_all, preferred_element_type=jnp.float32)
        d_query = jnp.concatenate([d_q_nope, d_q_rope], axis=-1).astype(jnp.bfloat16)
        dk_part = jnp.einsum("hqk,qhd->khd", d_score, q_nope, preferred_element_type=jnp.float32).astype(jnp.bfloat16)
        dv_part = jnp.einsum("hqk,qhd->khd", prob_b, d_out, preferred_element_type=jnp.float32).astype(jnp.bfloat16)
        dr_part = jnp.einsum("hqk,qhd->kd", d_score, q_rope, preferred_element_type=jnp.float32).astype(jnp.bfloat16)
        d_k_nope = lax.psum_scatter(dk_part, "cp", scatter_dimension=0, tiled=True)
        d_values = lax.psum_scatter(dv_part, "cp", scatter_dimension=0, tiled=True)
        d_key_rope = lax.psum_scatter(dr_part, "cp", scatter_dimension=0, tiled=True)
        d_latent = (jnp.einsum("thd,lhd->tl", d_k_nope, w_uk, preferred_element_type=jnp.float32)
                    + jnp.einsum("thd,lhd->tl", d_values, w_uv, preferred_element_type=jnp.float32)).astype(jnp.bfloat16)
        d_w_uk = lax.psum(jnp.einsum("tl,thd->lhd", latent, d_k_nope, preferred_element_type=jnp.float32), "cp")
        d_w_uv = lax.psum(jnp.einsum("tl,thd->lhd", latent, d_values, preferred_element_type=jnp.float32), "cp")
        return attn_out, d_query, d_latent, d_key_rope, d_w_uk, d_w_uv

    return jax.shard_map(local_step, mesh=mesh,
                         in_specs=(seq_spec, seq_spec, seq_spec, P(), P(), seq_spec),
                         out_specs=(seq_spec, seq_spec, seq_spec, seq_spec, P(), P()),
                         check_vma=False)
```

profile of v0, /device:TPU:17, one launch (start us, length us, event | category | flops | bytes accessed | tf_op | source)
XLA Modules:
  0.0 1012.2 jit_solution(2571052226530529102)
XLA Ops:
  7.2 3.1 fusion.24
  12.7 36.0 %all_gather.14 = bf16[4096,64]{0,1:T(8,128)(2,1)S(1)} all-gather(bf16[128,64]{0,1:T(8,128)(2,1)} %param.8), channel_id=1, replica_groups=mesh['cp'=32] {'cp'}, dimensions={0}, use_global_device_ids=true | all-gather | bytes 540672 | tf_op jit(solution)/shard_map/all_gather | solution.py:15
  49.1 78.1 %all-gather.5.cloned.1.call-done = bf16[4096,16,128]{2,0,1:T(8,128)(2,1)} async-done(((bf16[128,16,128]{2,0,1:T(8,128)(2,1)}), bf16[4096,16,128]{2,0,1:T(8,128)(2,1)}) %all-gather.5.cloned.1.call-update) | async-done | bytes 16777232 | tf_op jit(solution)/shard_map/all_gather | solution.py:13
  127.1 16.5 %fusion.46 = f32[16,4096,128]{2,1,0:T(8,128)} fusion(bf16[4096,16,128]{2,0,1:T(8,128)(2,1)} %all-gather.5.cloned.1.call-done, bf16[128,16,192]{0,2,1:T(8,128)(2,1)} %param.6), kind=kOutput, calls=%fused_computation.47 | convolution fusion | flops 2147483648 | bytes 50855936 | tf_op jit(solution)/shard_map/qhd,khd->hqk/dot_general | solution.py:29
  143.6 21.8 %fusion.55 = (f32[16,128]{1,0:T(8,128)S(1)}, f32[16,128,4096]{1,2,0:T(8,128)}) fusion(bf16[128,16,192]{0,2,1:T(8,128)(2,1)} %param.6, bf16[4096,64]{0,1:T(8,128)(2,1)S(1)} %all_gather.14, f32[16,4096,128]{2,1,0:T(8,128)} %fusion.46, pred[128,4096]{0,1:T(8,128)(4,1)S(1)} %iota_compare_fusion), kind=kOutput, calls=%fused_computation.58 | convolution fusion | flops 1107294208 | bytes 68427776 | tf_op jit(solution)/shard_map/qhd,kd->hqk/dot_general | solution.py:30
  165.4 13.0 %fusion.4 = f32[16,128]{1,0:T(8,128)S(1)} fusion(f32[16,128,4096]{1,2,0:T(8,128)} %get-tuple-element.21, f32[16,128]{1,0:T(8,128)S(1)} %get-tuple-element.20), kind=kLoop, calls=%fused_computation.9 | loop fusion | flops 16775168 | bytes 33570816 | tf_op jit(solution)/shard_map/reduce_sum | solution.py:40
  178.5 65.3 %all-gather.3.cloned.1.call-done = bf16[4096,16,128]{2,0,1:T(8,128)(2,1)} async-done(((bf16[128,16,128]{2,0,1:T(8,128)(2,1)}), bf16[4096,16,128]{2,0,1:T(8,128)(2,1)}) %all-gather.3.cloned.1.call-update) | async-done | bytes 16777232 | tf_op jit(solution)/shard_map/all_gather | solution.py:14
  243.8 20.2 %bitcast_convert_fusion = (f32[16,128,128]{1,2,0:T(8,128)}, bf16[16,128,128]{2,1,0:T(8,128)(2,1)}) fusion(bf16[4096,16,128]{2,0,1:T(8,128)(2,1)} %all-gather.3.cloned.1.call-done, f32[16,128,4096]{1,2,0:T(8,128)} %get-tuple-element.21, f32[16,128]{1,0:T(8,128)S(1)} %fusion.4, f32[16,128]{1,0:T(8,128)S(1)} %get-tuple-element.20), kind=kOutput, calls=%fused_computation.42 | convolution fusion | flops 2173173760 | bytes 51920896 | tf_op jit(solution)/shard_map/hqk,khd->qhd/dot_general | solution.py:43
  263.9 2.6 copy.55
  268.2 25.1 %fusion.1 = bf16[16,128,4096]{1,2,0:T(8,128)(2,1)} fusion(f32[16,128,4096]{1,2,0:T(8,128)} %get-tuple-element.21, f32[16,128]{1,0:T(8,128)S(1)} %copy.56, f32[16,128]{1,0:T(8,128)S(1)} %log_add_fusion, bf16[4096,16,128]{2,0,1:T(8,128)(2,1)} %all-gather.3.cloned.1.call-done, bf16[128,16,128]{2,1,0:T(8,128)(2,1)S(1)} %copy-done.1), kind=kOutput, calls=%fused_computation.2 | convolution fusion | flops 2189426688 | bytes 67649536 | tf_op jit(solution)/shard_map/qhd,khd->hqk/dot_general | solution.py:48
  293.3 11.5 %convert_bitcast_fusion.1 = bf16[4096,16,128]{2,0,1:T(8,128)(2,1)} fusion(bf16[16,128,4096]{1,2,0:T(8,128)(2,1)} %fusion.1, bf16[128,16,192]{0,2,1:T(8,128)(2,1)} %param.6), kind=kOutput, calls=%fused_computation.13 | convolution fusion | flops 2155872256 | bytes 34078720 | tf_op jit(solution)/shard_map/hqk,qhd->khd/dot_general | solution.py:54
  304.9 21.0 %convert_bitcast_fusion = bf16[4096,16,128]{2,0,1:T(8,128)(2,1)} fusion(f32[16,128,4096]{1,2,0:T(8,128)} %get-tuple-element.21, f32[16,128]{1,0:T(8,128)S(1)} %log_add_fusion, bf16[128,16,128]{2,1,0:T(8,128)(2,1)S(1)} %copy-done.1), kind=kOutput, calls=%fused_computation.12 | convolution fusion | flops 2172649472 | bytes 50864128 | tf_op jit(solution)/shard_map/hqk,qhd->khd/dot_general | solution.py:55
  326.0 10.9 %fusion.12 = bf16[4096,64]{0,1:T(8,128)(2,1)S(1)} fusion(bf16[16,128,4096]{1,2,0:T(8,128)(2,1)} %fusion.1, bf16[128,16,192]{0,2,1:T(8,128)(2,1)} %param.6), kind=kOutput, calls=%fused_computation.17 | convolution fusion | flops 1074003968 | bytes 17563648 | tf_op jit(solution)/shard_map/hqk,qhd->kd/dot_general | solution.py:56
  338.3 149.0 %reduce-scatter.6.cloned.1.call-done = bf16[128,16,128]{2,0,1:T(8,128)(2,1)} async-done(((bf16[4096,16,128]{2,0,1:T(8,128)(2,1)}), bf16[128,16,128]{2,0,1:T(8,128)(2,1)}) %reduce-scatter.6.cloned.1.call-update) | async-done | bytes 524304 | tf_op jit(solution)/shard_map/reduce_scatter | solution.py:57
  487.4 3.8 convolution_bitcast_fusion.2
  491.2 182.9 %reduce-scatter.8.cloned.1.call-done = bf16[128,16,128]{2,0,1:T(8,128)(2,1)} async-done(((bf16[4096,16,128]{2,0,1:T(8,128)(2,1)}), bf16[128,16,128]{2,0,1:T(8,128)(2,1)}) %reduce-scatter.8.cloned.1.call-update) | async-done | bytes 524304 | tf_op jit(solution)/shard_map/reduce_scatter | solution.py:58
  674.1 3.8 convolution_bitcast_fusion.1
  679.1 8.7 fusion.35
  687.8 13.3 %fusion.28 = bf16[128,16,128]{0,2,1:T(8,128)(2,1)S(1)} fusion(bf16[4096,16,128]{2,0,1:T(8,128)(2,1)} %all-gather.5.cloned.1.call-done, bf16[16,128,4096]{1,2,0:T(8,128)(2,1)} %fusion.1), kind=kOutput, calls=%fused_computation.33 | convolution fusion | flops 2147745792 | bytes 34078720 | tf_op jit(solution)/shard_map/hqk,khd->qhd/dot_general | solution.py:51
  702.1 79.8 %reduce-scatter.10.cloned.1.call-done = bf16[128,64]{1,0:T(8,128)(2,1)} async-done(((bf16[4096,64]{1,0:T(8,128)(2,1)}), bf16[128,64]{1,0:T(8,128)(2,1)}) %reduce-scatter.10.cloned.1.call-update) | async-done | bytes 16400
  785.3 3.1 fusion.39
  788.4 206.1 %all-reduce.3.cloned.1.call-done = (f32[512,16,128]{0,2,1:T(8,128)}, f32[512,16,128]{0,2,1:T(8,128)}) async-done(((f32[512,16,128]{0,2,1:T(8,128)}, f32[512,16,128]{0,2,1:T(8,128)}), (f32[512,16,128]{0,2,1:T(8,128)}, f32[512,16,128]{0,2,1:T(8,128)})) %all-reduce.3.cloned.1.call-update) | async-done | bytes 8388624 | tf_op jit(solution)/shard_map/psum | solution.py:62
  994.5 5.4 copy.46
  999.9 5.4 copy.47
  (33 shorter events, 11.4 us)
Async XLA Ops:
  7.2 3.2 copy-start
  7.2 120.0 %all-gather.5.cloned.1.call-start = ((), (), s32[]{:S(2)}) async-start(), calls=%async_computation.4 | async-start | bytes 17301504 | tf_op jit(solution)/shard_map/all_gather | solution.py:13
  10.3 233.4 %all-gather.3.cloned.1.call-start = ((), (), s32[]{:S(2)}) async-start(), calls=%async_computation.3 | async-start | bytes 17301504 | tf_op jit(solution)/shard_map/all_gather | solution.py:14
  12.6 474.8 %reduce-scatter.6.cloned.1.call-start = ((), (), s32[]{:S(2)}) async-start(), calls=%async_computation.5 | async-start | bytes 17301504 | tf_op jit(solution)/shard_map/reduce_scatter | solution.py:57
  178.5 88.1 %copy-start.1 = (bf16[128,16,128]{2,1,0:T(8,128)(2,1)S(1)}, bf16[128,16,128]{2,1,0:T(8,128)(2,1)}, u32[]{:S(2)}) copy-start(bf16[128,16,128]{2,1,0:T(8,128)(2,1)} %param.11) | copy-start | bytes 1572868
  304.8 369.2 %reduce-scatter.8.cloned.1.call-start = ((), (), s32[]{:S(2)}) async-start(), calls=%async_computation.6 | async-start | bytes 17301504 | tf_op jit(solution)/shard_map/reduce_scatter | solution.py:58
  325.9 161.5 %copy-start.3 = (bf16[128,512]{1,0:T(8,128)(2,1)S(1)}, bf16[128,512]{1,0:T(8,128)(2,1)}, u32[]{:S(2)}) copy-start(bf16[128,512]{1,0:T(8,128)(2,1)} %param.7) | copy-start | bytes 393220
  325.9 456.1 %reduce-scatter.10.cloned.1.call-start = ((), (), s32[]{:S(2)}) async-start(), calls=%async_computation.7 | async-start | bytes 1081344
  338.3 339.6 %copy-start.4 = (bf16[16,128,128]{2,1,0:T(8,128)(2,1)S(1)}, bf16[16,128,128]{2,1,0:T(8,128)(2,1)}, u32[]{:S(2)}) copy-start(bf16[16,128,128]{2,1,0:T(8,128)(2,1)} %get-tuple-element.23) | copy-start | bytes 1572868
  338.3 656.2 %all-reduce.3.cloned.1.call-start = ((), (), s32[]{:S(2)}) async-start(), calls=%async_computation.8 | async-start | bytes 16777216 | tf_op jit(solution)/shard_map/psum | solution.py:62
  687.8 97.5 %copy-start.2 = (bf16[128,16,128]{2,0,1:T(8,128)(2,1)S(1)}, bf16[128,16,128]{2,0,1:T(8,128)(2,1)}, u32[]{:S(2)}) copy-start(bf16[128,16,128]{2,0,1:T(8,128)(2,1)} %reduce-scatter.6.cloned.1.call-done) | copy-start | bytes 1572868
Sparse Core Ops, SparseCore 0:
  11.5 115.5 all-gather.4
  130.7 113.0 all-gather.2
  305.0 182.3 reduce-scatter.5
  489.5 184.5 reduce-scatter.7
  676.2 105.7 reduce-scatter.9
  788.3 206.1 all-reduce.2
where the time goes:
time: 1010 us
  waiting for transfers between devices  761 us (75%)
  matrix products  167 us (17%)
  blocking collectives  36 us (4%)
  local copies, waits for them, and re-layouts  17.6 us (2%)
  other arithmetic  15.9 us (2%)
  between operations  14.2 us (1%)
    psum x1, waiting for transfers between devices, local_step(): lax.psum(jnp.einsum('tl,thd->lhd', latent, d_k_nope, preferred_element_ty...  206 us
    reduce_scatter x1, waiting for transfers between devices, local_step(): d_values = lax.psum_scatter(dv_part, 'cp', scatter_dimension=0, tiled=True)  183 us
    reduce_scatter x1, waiting for transfers between devices, local_step(): d_k_nope = lax.psum_scatter(dk_part, 'cp', scatter_dimension=0, tiled=True)  149 us
    unnamed x7, waiting for transfers between devices  79.9 us
    all_gather x1, waiting for transfers between devices, gather_all(): k_all = lax.all_gather(k_nope, 'cp', tiled=True)  78.1 us
    all_gather x1, waiting for transfers between devices, gather_all(): v_all = lax.all_gather(values, 'cp', tiled=True)  65.3 us
    all_gather x1, blocking collectives, gather_all(): r_all = lax.all_gather(key_rope, 'cp', tiled=True)  36 us
    dot_general x1, matrix products, local_step(): jnp.einsum('qhd,khd->hqk', d_out, v_all, preferred_element_type=jnp.float32)  25.1 us
  transfers between devices with their start and end apart: 6, of which 6 were waited for; matrix products, arithmetic and copies ran while one was open for 12% of the time, Pallas kernels for 0%

commit v1 on v0

v1 whole, which is shorter than its diff:
```python
import functools
import math

import jax
import jax.numpy as jnp
from jax import lax
from jax.experimental import pallas as pl
from jax.experimental.pallas import tpu as pltpu
from jax.sharding import PartitionSpec as P

MESH = pl.DeviceIdType.MESH
NX, NY = 2, 2
BLK = 128
SUP = 256
CH = 1024
MSG = 320
CMSG = 576
NEG = -1e30
NT = (((1,), (1,)), ((), ()))
NN = (((1,), (0,)), ((), ()))


def mm(a, b, dims=NN):
    return lax.dot_general(a, b, dims, preferred_element_type=jnp.float32)


def unpack_rope(x):
    return jnp.concatenate([x[:, :64], x[:, 64:]], axis=0)


def pack_rope(x):
    return jnp.concatenate([x[:64], x[64:]], axis=1)


def kernel(nz, qk_dim, qd_ref, cr_ref, w_ref, wt_ref, od_recv, dkv_recv, dw_all,
           qd_recv, c_all, kr, v, kt, vt, s_buf, p_buf, ds_buf, dkr, dv, qf, dof, dot_, ot, dqt,
           od_send, dkv_out, dkv_part, dwt, dw_out, dw_part,
           q_send, q_rec, od_ssem, od_rsem, dkv_ssem, dkv_rsem, pair_sem,
           cg_rz, cg_rp, cg_sz, cg_sx, cg_sp, wg_rz, wg_rp, wg_sz, wg_sx, wg_sp):
    n_chip = NX * NY * nz
    n_dev = 2 * n_chip
    n_sup = n_chip // 2
    me = lax.axis_index("cp")
    chip, par = me // 2, me % 2
    partner = 2 * chip + (1 - par)
    x, y, z = chip % NX, (chip // NX) % NY, chip // (NX * NY)
    scale = 1.0 / math.sqrt(qk_dim)
    c1 = scale * math.log2(math.e)

    def chip_at(zq, yq, xq):
        return (zq * NY + yq) * NX + xq

    def col_chip(col, zq):
        return chip_at(zq, 1 - y if col >= 2 else y, 1 - x if col % 2 else x)

    def remote(src, dst, ssem, rsem, dev):
        return pltpu.make_async_remote_copy(src_ref=src, dst_ref=dst, send_sem=ssem, recv_sem=rsem,
                                            device_id=(dev,), device_id_type=MESH)

    def start(src, dst, ssem, rsem, dev):
        @pl.when(dev == me)
        def _():
            pltpu.make_async_copy(src, dst, rsem).start()

        @pl.when(dev != me)
        def _():
            remote(src, dst, ssem, rsem, dev).start()

    def sent(src, dst, ssem, rsem, dev):
        @pl.when(dev != me)
        def _():
            remote(src, dst, ssem, rsem, dev).wait_send()

    def arrived(dst, rsem):
        pltpu.make_async_copy(dst, dst, rsem).wait()

    barrier = pltpu.get_barrier_semaphore()

    def sig(i, carry):
        pl.semaphore_signal(barrier, inc=1, device_id=(lax.rem(me + i, n_dev),), device_id_type=MESH)
        return carry

    lax.fori_loop(1, n_dev, sig, 0)
    pl.semaphore_wait(barrier, n_dev - 1)

    def gather(buf, rows, rz, rp, sz, sx, sp, background):
        half = rows // 2
        dev_z = lambda zq: 2 * chip_at(zq, y, x) + par
        dev_x = 2 * chip_at(z, y, 1 - x) + par
        dev_y = 2 * chip_at(z, 1 - y, x) + par

        def blk(col, zq):
            return buf.at[par, col_chip(col, zq)]

        def up(zq):
            return remote(blk(0, zq), blk(0, zq), sz.at[0, zq], rz.at[0, zq, 0], dev_z(jnp.minimum(z + 1, nz - 1)))

        def down(zq):
            return remote(blk(0, zq), blk(0, zq), sz.at[1, zq], rz.at[0, zq, 0], dev_z(jnp.maximum(z - 1, 0)))

        def to_x(zq):
            return remote(blk(0, zq), blk(0, zq), sx.at[0, zq], rz.at[1, zq, 0], dev_x)

        def to_y(zq):
            return remote(blk(0, zq), blk(0, zq), sx.at[1, zq], rz.at[2, zq, 0], dev_y)

        def half_y(zq):
            b = blk(1, zq).at[pl.ds(0, half)]
            return remote(b, b, sx.at[2, zq], rz.at[3, zq, 0], dev_y)

        def half_x(zq):
            b = blk(2, zq).at[pl.ds(half, half)]
            return remote(b, b, sx.at[3, zq], rz.at[3, zq, 1], dev_x)

        def pair(col, zq):
            return remote(blk(col, zq), blk(col, zq), sp.at[col, zq], rp.at[col, zq], partner)

        def own_col(zq):
            to_x(zq).start()
            to_y(zq).start()
            pair(0, zq).start()

        def xy_wait1(zq):
            remote(blk(1, zq), blk(1, zq), sx.at[0, zq], rz.at[1, zq, 0], dev_x).wait_recv()
            half_y(zq).start()
            pair(1, zq).start()
            remote(blk(2, zq), blk(2, zq), sx.at[1, zq], rz.at[2, zq, 0], dev_y).wait_recv()
            half_x(zq).start()
            pair(2, zq).start()

        def diag(zq):
            b0 = blk(3, zq).at[pl.ds(0, half)]
            b1 = blk(3, zq).at[pl.ds(half, half)]
            remote(b0, b0, sx.at[2, zq], rz.at[3, zq, 0], dev_y).wait_recv()
            remote(b1, b1, sx.at[3, zq], rz.at[3, zq, 1], dev_x).wait_recv()
            pair(3, zq).start()

        def dist(d, f):
            if d == 0:
                f(z)
                return

            @pl.when(z - d >= 0)
            def _():
                f(z - d)

            @pl.when(z + d < nz)
            def _():
                f(z + d)

        @pl.when(z + 1 < nz)
        def _():
            up(z).start()

        @pl.when(z > 0)
        def _():
            down(z).start()

        own_col(z)
        background(0)
        for d in range(1, nz):
            @pl.when(z - d >= 0)
            def _():
                remote(blk(0, z - d), blk(0, z - d), sz.at[0, z - d], rz.at[0, z - d, 0], partner).wait_recv()

                @pl.when(z + 1 < nz)
                def _():
                    up(z - d).start()

                own_col(z - d)

            @pl.when(z + d < nz)
            def _():
                remote(blk(0, z + d), blk(0, z + d), sz.at[1, z + d], rz.at[0, z + d, 0], partner).wait_recv()

                @pl.when(z > 0)
                def _():
                    down(z + d).start()

                own_col(z + d)

            dist(d - 1, xy_wait1)
            background(d)
            if d >= 2:
                dist(d - 2, diag)
        dist(nz - 1, xy_wait1)
        background(nz)
        for d in range(max(nz - 2, 0), nz):
            dist(d, diag)

        def finish():
            for zq in range(nz):
                for col in range(4):
                    pair(col, zq).wait()
                for c in (to_x, to_y, half_y, half_x):
                    c(zq).wait_send()

                @pl.when(jnp.logical_and(z >= zq, z + 1 < nz))
                def _():
                    up(zq).wait_send()

                @pl.when(jnp.logical_and(z <= zq, z > 0))
                def _():
                    down(zq).wait_send()

        return finish

    owner_core = lax.rem((chip + 1) // 2, 2)
    q_slot = 2 * (chip // 2) + par

    def q_copy(i):
        head = lax.rem(chip + i, n_chip)
        return qd_ref.at[head], qd_recv.at[q_slot], q_send.at[i], q_rec.at[q_slot], 2 * head + owner_core

    def run_parts(copy, parts):
        per = -(-n_chip // parts)

        def background(step):
            def go(i, carry):
                start(*copy(i))
                return carry

            lax.fori_loop(min(step * per, n_chip), min((step + 1) * per, n_chip), go, 0)

        return background

    c_all[par, chip] = cr_ref[...]
    finish_c = gather(c_all, CMSG, cg_rz, cg_rp, cg_sz, cg_sx, cg_sp, run_parts(q_copy, nz + 1))

    dkr[...] = jnp.zeros_like(dkr)
    dv[...] = jnp.zeros_like(dv)
    finish_c()

    def latent_of(ch):
        rows = []
        for q in range(2):
            rows.append(jnp.concatenate([c_all[q, ch, pl.ds(BLK * i, BLK), :] for i in range(4)], axis=1))
        return jnp.concatenate(rows, axis=0)

    def up_project(ch, carry):
        base = pl.multiple_of(ch * SUP, SUP)
        lat = latent_of(ch)
        kv = mm(lat, w_ref[...]).astype(jnp.bfloat16)
        kvt = mm(wt_ref[...], lat, NT).astype(jnp.bfloat16)
        kr[pl.ds(base, SUP), pl.ds(0, 128)] = kv[:, :128]
        v[pl.ds(base, SUP), :] = kv[:, 128:]
        kt[pl.ds(0, 128), pl.ds(base, SUP)] = kvt[:128]
        vt[:, pl.ds(base, SUP)] = kvt[128:]
        for q in range(2):
            rp = c_all[q, ch, pl.ds(4 * BLK, 64), :].astype(jnp.float32)
            r = unpack_rope(rp)
            kr[pl.ds(base + q * BLK, BLK), pl.ds(128, 128)] = jnp.concatenate(
                [r, jnp.zeros_like(r)], axis=1).astype(jnp.bfloat16)
            rt = jnp.transpose(r)
            kt[pl.ds(128, 64), pl.ds(base + q * BLK, BLK)] = rt.astype(jnp.bfloat16)
        return carry

    lax.fori_loop(0, n_chip, up_project, 0)

    k_iota = lax.broadcasted_iota(jnp.int32, (SUP, SUP), 0)
    q_iota = lax.broadcasted_iota(jnp.int32, (SUP, SUP), 1)
    diff = k_iota - q_iota

    def od_copy(s, i):
        ch = 2 * s + lax.rem(s + par, 2)
        return od_send.at[2 * s + i], od_recv.at[chip], od_ssem.at[2 * s + i], od_rsem.at[chip], 2 * ch + i

    def superblock(s, carry):
        ch = 2 * s + lax.rem(s + par, 2)
        for i in range(2):
            slot = 2 * s + i
            arrived(qd_recv.at[slot], q_rec.at[slot])
            rows = pl.ds(i * BLK, BLK)
            qf[rows, pl.ds(0, 128)] = qd_recv[slot, pl.ds(0, BLK), :]
            qr = unpack_rope(qd_recv[slot, pl.ds(2 * BLK, 64), :].astype(jnp.float32))
            qf[rows, pl.ds(128, 128)] = jnp.concatenate([qr, jnp.zeros_like(qr)], axis=1).astype(jnp.bfloat16)
            do = qd_recv[slot, pl.ds(BLK, BLK), :]
            dof[rows, :] = do
            dot_[:, rows] = jnp.transpose(do.astype(jnp.float32))
        n_ch = s // (CH // (2 * SUP)) + 1

        def score(j, m8):
            for t in range(CH // SUP):
                r0 = pl.multiple_of(j * CH + t * SUP, SUP)
                st = mm(kr[pl.ds(r0, SUP), :], qf[...], NT)
                st = jnp.where(diff <= ch * SUP - r0, st, NEG)
                s_buf[pl.ds(r0, SUP), :] = st
                m8 = jnp.maximum(m8, jnp.max(st.reshape(SUP // 8, 8, SUP), axis=0))
            return m8

        m8 = lax.fori_loop(0, n_ch, score, jnp.full((8, SUP), NEG, jnp.float32))
        m2 = jnp.max(m8, axis=0, keepdims=True) * c1
        ot[...] = jnp.zeros_like(ot)

        def forward(j, l8):
            base = pl.multiple_of(j * CH, CH)
            for t in range(CH // SUP):
                p = jnp.exp2(s_buf[pl.ds(base + t * SUP, SUP), :] * c1 - m2)
                l8 = l8 + jnp.sum(p.reshape(SUP // 8, 8, SUP), axis=0)
                p_buf[pl.ds(t * SUP, SUP), :] = p.astype(jnp.bfloat16)
            ot[...] += mm(vt[:, pl.ds(base, CH)], p_buf[...])
            return l8

        l8 = lax.fori_loop(0, n_ch, forward, jnp.zeros((8, SUP), jnp.float32))
        l = jnp.sum(l8, axis=0, keepdims=True)
        o = ot[...] / l
        lse2 = m2 + jnp.log2(l)
        delta = jnp.sum(o * dot_[...], axis=0, keepdims=True)
        o_rows = jnp.transpose(o)
        for i in range(2):
            od_send[2 * s + i, pl.ds(0, BLK), :] = o_rows[i * BLK:(i + 1) * BLK].astype(jnp.bfloat16)
        dqt[...] = jnp.zeros_like(dqt)

        def backward(j, carry):
            base = pl.multiple_of(j * CH, CH)
            for t in range(CH // SUP):
                rows = pl.ds(base + t * SUP, SUP)
                dp = mm(v[rows, :], dof[...], NT)
                p = jnp.exp2(s_buf[rows, :] * c1 - lse2)
                p_buf[pl.ds(t * SUP, SUP), :] = p.astype(jnp.bfloat16)
                ds_buf[pl.ds(t * SUP, SUP), :] = (p * (dp - delta) * scale).astype(jnp.bfloat16)
            for t in range(CH // SUP):
                rows = pl.ds(base + t * SUP, SUP)
                dkr[rows, :] += mm(ds_buf[pl.ds(t * SUP, SUP), :], qf[...])
                dv[rows, :] += mm(p_buf[pl.ds(t * SUP, SUP), :], dof[...])
            dqt[...] += mm(kt[:, pl.ds(base, CH)], ds_buf[...])
            return carry

        lax.fori_loop(0, n_ch, backward, 0)
        dq_n = jnp.transpose(dqt[pl.ds(0, 128), :])
        dq_r = jnp.transpose(dqt[pl.ds(128, 64), :])
        for i in range(2):
            od_send[2 * s + i, pl.ds(BLK, BLK), :] = dq_n[i * BLK:(i + 1) * BLK].astype(jnp.bfloat16)
            od_send[2 * s + i, pl.ds(2 * BLK, 64), :] = pack_rope(dq_r[i * BLK:(i + 1) * BLK]).astype(jnp.bfloat16)
        for i in range(2):
            start(*od_copy(s, i))
        return carry

    lax.fori_loop(0, n_sup, superblock, 0)

    dwt[...] = jnp.zeros_like(dwt)

    def finish_keys(ch, carry):
        base = pl.multiple_of(ch * SUP, SUP)
        for q in range(2):
            rows = pl.ds(base + q * BLK, BLK)
            dkv_out[q, ch, pl.ds(0, BLK), :] = dkr[rows, pl.ds(0, 128)].astype(jnp.bfloat16)
            dkv_out[q, ch, pl.ds(BLK, BLK), :] = dv[rows, :].astype(jnp.bfloat16)
            dkv_out[q, ch, pl.ds(2 * BLK, 64), :] = pack_rope(dkr[rows, pl.ds(128, 128)][:, :64]).astype(jnp.bfloat16)
        dk_t = jnp.transpose(dkr[pl.ds(base, SUP), pl.ds(0, 128)])
        dv_t = jnp.transpose(dv[pl.ds(base, SUP), :])
        dkv_t = jnp.concatenate([dk_t, dv_t], axis=0).astype(jnp.bfloat16)
        dwt[...] += mm(dkv_t, latent_of(ch))
        return carry

    lax.fori_loop(0, n_chip, finish_keys, 0)
    pair_dkv = remote(dkv_out.at[1 - par], dkv_part, pair_sem.at[0], pair_sem.at[1], partner)
    pair_dkv.start()
    for q in range(2):
        dw_out[q] = jnp.transpose(dwt[pl.ds(q * 128, 128), :])
    pair_dw = remote(dw_out.at[1 - par], dw_part, pair_sem.at[2], pair_sem.at[3], partner)
    pair_dw.start()
    pair_dkv.wait()

    def add_pair(ch, carry):
        dkv_out[par, ch] = (dkv_out[par, ch].astype(jnp.float32) + dkv_part[ch].astype(jnp.float32)).astype(jnp.bfloat16)
        return carry

    lax.fori_loop(0, n_chip, add_pair, 0)
    pair_dw.wait()
    dw_all[par, chip] = dw_out[par] + dw_part[...]

    def dkv_copy(i):
        ch = lax.rem(chip + i, n_chip)
        return dkv_out.at[par, ch], dkv_recv.at[chip], dkv_ssem.at[i], dkv_rsem.at[chip], 2 * ch + par

    finish_w = gather(dw_all, 512, wg_rz, wg_rp, wg_sz, wg_sx, wg_sp, run_parts(dkv_copy, nz + 1))
    finish_w()

    def drain(i, carry):
        sent(*q_copy(i))
        sent(*dkv_copy(i))
        sent(*od_copy(i // 2, i % 2))
        arrived(od_recv.at[i], od_rsem.at[i])
        arrived(dkv_recv.at[i], dkv_rsem.at[i])
        return carry

    lax.fori_loop(0, n_chip, drain, 0)


def solution(mesh):
    n_dev = mesh.shape["cp"]
    n_chip = n_dev // 2
    nz = n_chip // (NX * NY)
    seq = n_dev * BLK
    seq_spec = P("cp")

    def local_step(queries, latent, key_rope, w_uk, w_uv, d_out):
        head = lax.axis_index("cp") // 2
        q_n = queries[:, :, :128].transpose(1, 0, 2)
        q_r = queries[:, :, 128:].transpose(1, 0, 2)
        q_r = jnp.concatenate([q_r[:, :64], q_r[:, 64:]], axis=2)
        qd = jnp.concatenate([q_n, d_out.transpose(1, 0, 2), q_r], axis=1)
        r2 = jnp.concatenate([key_rope[:64], key_rope[64:]], axis=1)
        cr = jnp.concatenate([latent[:, 128 * i:128 * (i + 1)] for i in range(4)] + [r2], axis=0)
        wk = lax.dynamic_index_in_dim(w_uk, head, 1, keepdims=False)
        wv = lax.dynamic_index_in_dim(w_uv, head, 1, keepdims=False)
        w = jnp.concatenate([wk, wv], axis=1)
        bf, f32 = jnp.bfloat16, jnp.float32
        vm = pl.BlockSpec(memory_space=pltpu.VMEM)
        dma = pltpu.SemaphoreType.DMA
        gather_sems = [dma((4, nz, 2)), dma((4, nz)), dma((2, nz)), dma((4, nz)), dma((4, nz))]
        od, dkv, dw = pl.pallas_call(
            functools.partial(kernel, nz, queries.shape[-1]),
            out_shape=(jax.ShapeDtypeStruct((n_chip, MSG, 128), bf),
                       jax.ShapeDtypeStruct((n_chip, MSG, 128), bf),
                       jax.ShapeDtypeStruct((2, n_chip, 512, 128), f32)),
            in_specs=[vm] * 4,
            out_specs=(vm, vm, vm),
            scratch_shapes=[
                pltpu.VMEM((n_chip, MSG, 128), bf),
                pltpu.VMEM((2, n_chip, CMSG, 128), bf),
                pltpu.VMEM((seq, 256), bf),
                pltpu.VMEM((seq, 128), bf),
                pltpu.VMEM((192, seq), bf),
                pltpu.VMEM((128, seq), bf),
                pltpu.VMEM((seq, SUP), f32),
                pltpu.VMEM((CH, SUP), bf),
                pltpu.VMEM((CH, SUP), bf),
                pltpu.VMEM((seq, 256), f32),
                pltpu.VMEM((seq, 128), f32),
                pltpu.VMEM((SUP, 256), bf),
                pltpu.VMEM((SUP, 128), bf),
                pltpu.VMEM((128, SUP), f32),
                pltpu.VMEM((128, SUP), f32),
                pltpu.VMEM((192, SUP), f32),
                pltpu.VMEM((n_chip, MSG, 128), bf),
                pltpu.VMEM((2, n_chip, MSG, 128), bf),
                pltpu.VMEM((n_chip, MSG, 128), bf),
                pltpu.VMEM((256, 512), f32),
                pltpu.VMEM((2, 512, 128), f32),
                pltpu.VMEM((512, 128), f32),
                dma((n_chip,)), dma((n_chip,)), dma((n_chip,)), dma((n_chip,)), dma((n_chip,)), dma((n_chip,)),
                dma((4,)),
            ] + gather_sems + gather_sems,
            compiler_params=pltpu.CompilerParams(
                collective_id=0, has_side_effects=True, vmem_limit_bytes=60 * 1024 * 1024),
        )(qd, cr, w, w.T)
        attn_out = od[:, :BLK].transpose(1, 0, 2)
        dq_r = od[:, 2 * BLK:]
        dq_r = jnp.concatenate([dq_r[:, :, :64], dq_r[:, :, 64:]], axis=1)
        d_query = jnp.concatenate([od[:, BLK:2 * BLK], dq_r], axis=2).transpose(1, 0, 2)
        d_latent = (jnp.einsum("htd,lhd->tl", dkv[:, :BLK], w_uk, preferred_element_type=f32)
                    + jnp.einsum("htd,lhd->tl", dkv[:, BLK:2 * BLK], w_uv, preferred_element_type=f32)).astype(bf)
        dr = jnp.sum(dkv[:, 2 * BLK:].astype(f32), axis=0)
        d_key_rope = jnp.concatenate([dr[:, :64], dr[:, 64:]], axis=0).astype(bf)
        return (attn_out, d_query, d_latent, d_key_rope,
                dw[0].transpose(1, 0, 2), dw[1].transpose(1, 0, 2))

    return jax.shard_map(local_step, mesh=mesh,
                         in_specs=(seq_spec, seq_spec, seq_spec, P(), P(), seq_spec),
                         out_specs=(seq_spec, seq_spec, seq_spec, seq_spec, P(), P()),
                         check_vma=False)
```

time: 1010 us -> 199 us (0.20)
  the two profiles are of different devices: /device:TPU:17 before, /device:TPU:5 now
where the time goes in v1:
time: 199 us; the launch traced here: 198 us
  Pallas kernels  167 us (84%)
  local copies, waits for them, and re-layouts  24.5 us (12%)
  matrix products  4.06 us (2%)
  other arithmetic  2.41 us (1%)
    pallas_call x1, Pallas kernels, local_step(): pl.pallas_call(functools.partial(kernel, nz, queries.shape[-1]), out_shap...  167 us
    unnamed x26, local copies, waits for them, and re-layouts  12.9 us
    transpose x1, local copies, waits for them, and re-layouts, local_step(): dw[1].transpose(1, 0, 2)  4.03 us

profile of v1, /device:TPU:5, one launch (start us, length us, event | category | flops | bytes accessed | tf_op | source)
XLA Modules:
  0.0 198.5 jit_solution(4667663554608089212)
XLA Ops:
  0.6 1.0 slice.69
  1.7 0.3 copy.42
  2.0 0.1 copy.58
  2.2 0.6 slice-done
  2.7 0.3 copy.41
  3.0 1.3 maximum_maximum_fusion.qd_ref
  4.6 0.1 copy.43
  4.8 2.1 %constant_dynamic-slice_fusion = (bf16[512,1,128]{2,1,0:T(2,128)(2,1)S(1)}, bf16[512,1,128]{2,1,0:T(2,128)(2,1)S(1)}) fusion(bf16[512,16,128]{2,1,0:T(8,128)(2,1)} %param.10, s32[]{:T(128)S(6)} %select_n.11, bf16[512,16,128]{2,1,0:T(8,128)(2,1)} %param.9), kind=kLoop, calls=%fused_computation.24 | loop fusion | bytes 524292 | tf_op jit(solution)/shard_map/jit(dynamic_index_in_dim)/dynamic_slice | solution.py:407
  6.9 0.1 copy.32
  7.1 0.1 copy.31
  7.2 0.7 fusion.18
  8.0 0.8 copy.33.w_ref
  8.8 166.7 %shard_map.109 = (bf16[16,320,128]{2,1,0:T(8,128)(2,1)}, bf16[16,320,128]{2,1,0:T(8,128)(2,1)}, f32[2,16,512,128]{3,2,1,0:T(8,128)}) custom-call(bf16[16,320,128]{2,1,0:T(8,128)(2,1)} %maximum_maximum_fusion.qd_ref, bf16[576,128]{1,0:T(8,128)(2,1)} %copy-done.1, bf16[512,256]{1,0:T(8,128)(2,1)} %copy.33.w_ref, bf16[256,512]{1,0:T(8,128)(2,1)} %get-tuple-element.32.wt_ref), custom_call_target="tpu_custom_call" | custom-call | tf_op jit(solution)/shard_map/pallas_call | solution.py:413
  175.5 1.3 fusion.19
  176.8 1.1 copy.36
  178.0 1.2 fusion.20
  179.2 0.2 maximum_bitcast_fusion
  179.4 1.3 copy.37
  180.7 2.6 %fusion.4 = f32[128,512]{1,0:T(8,128)S(1)} fusion(bf16[512,16,128]{2,1,0:T(8,128)(2,1)} %param.9, bf16[16,320,128]{2,1,0:T(8,128)(2,1)S(1)} %copy-done.4), kind=kOutput, calls=%fused_computation.7 | convolution fusion | flops 268435456 | bytes 2883584 | tf_op jit(solution)/shard_map/htd,lhd->tl/dot_general | solution.py:453
  183.2 1.5 fusion.13
  184.9 0.7 copy.38
  185.6 4.0 %slice_bitcast_fusion = (f32[512,16,128]{2,0,1:T(8,128)S(1)}, f32[512,16,128]{2,0,1:T(8,128)S(1)}) fusion(f32[2,16,512,128]{3,2,1,0:T(8,128)} %get-tuple-element.11), kind=kLoop, calls=%fused_computation | loop fusion | bytes 16777216 | tf_op jit(solution)/shard_map/transpose | solution.py:458
  189.6 4.4 %copy.39 = f32[512,16,128]{2,1,0:T(8,128)} copy(f32[512,16,128]{2,0,1:T(8,128)S(1)} %get-tuple-element.25) | data formatting | bytes 8388608
  194.1 4.4 %copy.40 = f32[512,16,128]{2,1,0:T(8,128)} copy(f32[512,16,128]{2,0,1:T(8,128)S(1)} %get-tuple-element.24) | data formatting | bytes 8388608
  (24 shorter events, 0.5 us)
Async XLA Ops:
  0.6 1.4 copy-start
  1.7 1.1 slice-start
  2.7 1.6 copy-start.2
  2.7 1.7 copy-start.3
  4.8 4.0 %copy-start.1 = (bf16[576,128]{1,0:T(8,128)(2,1)}, bf16[576,128]{1,0:T(8,128)(2,1)S(1)}, u32[]{:S(2)}) copy-start(bf16[576,128]{1,0:T(8,128)(2,1)S(1)} %maximum_dynamic-update-slice_fusion.cr_ref) | copy-start | bytes 442372
  179.2 1.5 copy-start.4
  180.7 2.6 %copy-start.5 = (bf16[512,16,128]{2,1,0:T(8,128)(2,1)S(1)}, bf16[512,16,128]{2,1,0:T(8,128)(2,1)}, u32[]{:S(2)}) copy-start(bf16[512,16,128]{2,1,0:T(8,128)(2,1)} %param.10) | copy-start | bytes 6291460

commit v2 on v1

v2 whole, which is shorter than its diff:
```python
import functools
import math

import jax
import jax.numpy as jnp
from jax import lax
from jax.experimental import pallas as pl
from jax.experimental.pallas import tpu as pltpu
from jax.sharding import PartitionSpec as P

MESH = pl.DeviceIdType.MESH
NX, NY = 2, 2
BLK = 128
SUP = 256
CH = 1024
MSG = 320
CMSG = 576
NEG = -1e30
NT = (((1,), (1,)), ((), ()))
NN = (((1,), (0,)), ((), ()))


def mm(a, b, dims=NN):
    return lax.dot_general(a, b, dims, preferred_element_type=jnp.float32)


def unpack_rope(x):
    return jnp.concatenate([x[:, :64], x[:, 64:]], axis=0)


def pack_rope(x):
    return jnp.concatenate([x[:64], x[64:]], axis=1)


def kernel(nz, qk_dim, qd_ref, cr_ref, wk_ref, wv_ref, o_out, dq_out, dkv_recv, dwk_out, dwv_out,
           od_recv, dw_all, w_cat, wt_cat, qd_recv, c_all, kr, v, kt, vt, s_buf, p_buf, ds_buf, dkr, dv, qt, dof, dot_, ot, dqt,
           od_send, dkv_out, dkv_part, dwt, dw_out, dw_part,
           q_send, q_rec, od_ssem, od_rsem, dkv_ssem, dkv_rsem, pair_sem, dw_sem,
           cg_rz, cg_rp, cg_sz, cg_sx, cg_sp, wg_rz, wg_rp, wg_sz, wg_sx, wg_sp):
    n_chip = NX * NY * nz
    n_dev = 2 * n_chip
    n_sup = n_chip // 2
    me = lax.axis_index("cp")
    chip, par = me // 2, me % 2
    partner = 2 * chip + (1 - par)
    x, y, z = chip % NX, (chip // NX) % NY, chip // (NX * NY)
    scale = 1.0 / math.sqrt(qk_dim)
    c1 = scale * math.log2(math.e)

    def chip_at(zq, yq, xq):
        return (zq * NY + yq) * NX + xq

    def col_chip(col, zq):
        return chip_at(zq, 1 - y if col >= 2 else y, 1 - x if col % 2 else x)

    def remote(src, dst, ssem, rsem, dev):
        return pltpu.make_async_remote_copy(src_ref=src, dst_ref=dst, send_sem=ssem, recv_sem=rsem,
                                            device_id=(dev,), device_id_type=MESH)

    def start(src, dst, ssem, rsem, dev):
        @pl.when(dev == me)
        def _():
            pltpu.make_async_copy(src, dst, rsem).start()

        @pl.when(dev != me)
        def _():
            remote(src, dst, ssem, rsem, dev).start()

    def sent(src, dst, ssem, rsem, dev):
        @pl.when(dev != me)
        def _():
            remote(src, dst, ssem, rsem, dev).wait_send()

    def arrived(dst, rsem):
        pltpu.make_async_copy(dst, dst, rsem).wait()

    barrier = pltpu.get_barrier_semaphore()

    def sig(i, carry):
        pl.semaphore_signal(barrier, inc=1, device_id=(lax.rem(me + i, n_dev),), device_id_type=MESH)
        return carry

    lax.fori_loop(1, n_dev, sig, 0)
    pl.semaphore_wait(barrier, n_dev - 1)

    def gather(buf, rows, chain, rz, rp, sz, sx, sp, background, ready):
        half = rows // 2
        dev_z = lambda zq: 2 * chip_at(zq, y, x) + par
        dev_x = 2 * chip_at(z, y, 1 - x) + par
        dev_y = 2 * chip_at(z, 1 - y, x) + par

        def blk(col, zq):
            return buf.at[par, col_chip(col, zq)]

        def along_z(zq, to, k):
            return remote(blk(0, zq), blk(0, zq), sz.at[k, zq], rz.at[0, zq, 0], dev_z(to))

        def to_x(col, zq):
            return remote(blk(col, zq), blk(col, zq), sx.at[0, zq], rz.at[1, zq, 0], dev_x)

        def to_y(col, zq):
            return remote(blk(col, zq), blk(col, zq), sx.at[1, zq], rz.at[2, zq, 0], dev_y)

        def half_y(col, zq):
            b = blk(col, zq).at[pl.ds(0, half)]
            return remote(b, b, sx.at[2, zq], rz.at[3, zq, 0], dev_y)

        def half_x(col, zq):
            b = blk(col, zq).at[pl.ds(half, half)]
            return remote(b, b, sx.at[3, zq], rz.at[3, zq, 1], dev_x)

        def pair(col, zq):
            return remote(blk(col, zq), blk(col, zq), sp.at[col, zq], rp.at[col, zq], partner)

        def own_col(zq):
            to_x(0, zq).start()
            to_y(0, zq).start()
            pair(0, zq).start()

        def xy(zq):
            to_x(1, zq).wait_recv()
            half_y(1, zq).start()
            pair(1, zq).start()
            to_y(2, zq).wait_recv()
            half_x(2, zq).start()
            pair(2, zq).start()

        def diag(zq):
            half_y(3, zq).wait_recv()
            half_x(3, zq).wait_recv()
            pair(3, zq).start()
            for col in range(4):
                pair(col, zq).wait_recv()
            ready(zq)

        def dist(d, f):
            if d == 0:
                f(z)
                return

            @pl.when(z - d >= 0)
            def _():
                f(z - d)

            @pl.when(z + d < nz)
            def _():
                f(z + d)

        def z_sends(go):
            if chain:
                for zq in range(nz):
                    @pl.when(jnp.logical_and(z >= zq, z + 1 < nz))
                    def _():
                        go(along_z(zq, z + 1, 0))

                    @pl.when(jnp.logical_and(z <= zq, z > 0))
                    def _():
                        go(along_z(zq, z - 1, 1))
            else:
                for d in range(1, nz):
                    @pl.when(z + d < nz)
                    def _():
                        go(along_z(z, z + d, d - 1))

                    @pl.when(z - d >= 0)
                    def _():
                        go(along_z(z, z - d, nz - 2 + d))

        if chain:
            @pl.when(z + 1 < nz)
            def _():
                along_z(z, z + 1, 0).start()

            @pl.when(z > 0)
            def _():
                along_z(z, z - 1, 1).start()
        else:
            z_sends(lambda c: c.start())

        own_col(z)
        background(0)
        for d in range(1, nz):
            @pl.when(z - d >= 0)
            def _():
                along_z(z - d, z, 0).wait_recv()
                if chain:
                    @pl.when(z + 1 < nz)
                    def _():
                        along_z(z - d, z + 1, 0).start()

                own_col(z - d)

            @pl.when(z + d < nz)
            def _():
                along_z(z + d, z, 1).wait_recv()
                if chain:
                    @pl.when(z > 0)
                    def _():
                        along_z(z + d, z - 1, 1).start()

                own_col(z + d)

            dist(d - 1, xy)
            background(d)
            if d >= 2:
                dist(d - 2, diag)
        dist(nz - 1, xy)
        background(nz)
        for d in range(max(nz - 2, 0), nz):
            dist(d, diag)

        def finish():
            z_sends(lambda c: c.wait_send())
            for zq in range(nz):
                for col in range(4):
                    pair(col, zq).wait_send()
                to_x(0, zq).wait_send()
                to_y(0, zq).wait_send()
                half_y(1, zq).wait_send()
                half_x(2, zq).wait_send()

        return finish

    owner_core = lax.rem((chip + 1) // 2, 2)
    q_slot = 2 * (chip // 2) + par

    def q_copy(i):
        head = lax.rem(chip + i, n_chip)
        return qd_ref.at[head], qd_recv.at[q_slot], q_send.at[i], q_rec.at[q_slot], 2 * head + owner_core

    def latent_of(ch):
        rows = []
        for q in range(2):
            rows.append(jnp.concatenate([c_all[q, ch, pl.ds(BLK * i, BLK), :] for i in range(4)], axis=1))
        return jnp.concatenate(rows, axis=0)

    def up_project(ch, carry):
        base = pl.multiple_of(ch * SUP, SUP)
        lat = latent_of(ch)
        kv = mm(lat, w_cat[...]).astype(jnp.bfloat16)
        kvt = mm(wt_cat[...], lat, NT).astype(jnp.bfloat16)
        kr[pl.ds(base, SUP), pl.ds(0, 128)] = kv[:, :128]
        v[pl.ds(base, SUP), :] = kv[:, 128:]
        kt[pl.ds(0, 128), pl.ds(base, SUP)] = kvt[:128]
        vt[:, pl.ds(base, SUP)] = kvt[128:]
        for q in range(2):
            rt = c_all[q, ch, pl.ds(4 * BLK, 64), :]
            kt[pl.ds(128, 64), pl.ds(base + q * BLK, BLK)] = rt
            r = jnp.transpose(rt.astype(jnp.float32))
            kr[pl.ds(base + q * BLK, BLK), pl.ds(128, 128)] = jnp.concatenate(
                [r, jnp.zeros_like(r)], axis=1).astype(jnp.bfloat16)
        return carry

    def up_column(zq):
        lax.fori_loop(0, 4, lambda i, carry: up_project(zq * 4 + i, carry), 0)

    def send_q(step):
        if step == 0:
            def go(i, carry):
                start(*q_copy(i))
                return carry

            lax.fori_loop(0, n_chip, go, 0)
            dkr[...] = jnp.zeros_like(dkr)
            dv[...] = jnp.zeros_like(dv)
            w_cat[...] = jnp.concatenate([wk_ref[...], wv_ref[...]], axis=1)
            for i, w in enumerate((wk_ref, wv_ref)):
                wt_cat[pl.ds(i * 128, 128), :] = jnp.transpose(w[...].astype(jnp.float32)).astype(jnp.bfloat16)
            qt[pl.ds(192, 64), :] = jnp.zeros((64, SUP), jnp.bfloat16)

    c_all[par, chip] = cr_ref[...]
    finish_c = gather(c_all, CMSG, False, cg_rz, cg_rp, cg_sz, cg_sx, cg_sp, send_q, up_column)


    k_iota = lax.broadcasted_iota(jnp.int32, (SUP, SUP), 0)
    q_iota = lax.broadcasted_iota(jnp.int32, (SUP, SUP), 1)
    diff = k_iota - q_iota

    def od_copy(s, i):
        ch = 2 * s + lax.rem(s + par, 2)
        return od_send.at[2 * s + i], od_recv.at[chip], od_ssem.at[2 * s + i], od_rsem.at[chip], 2 * ch + i

    def superblock(s, carry):
        ch = 2 * s + lax.rem(s + par, 2)
        for i in range(2):
            slot = 2 * s + i
            arrived(qd_recv.at[slot], q_rec.at[slot])
            rows = pl.ds(i * BLK, BLK)
            qt[pl.ds(0, 192), rows] = qd_recv[slot, pl.ds(0, 192), :]
            do = qd_recv[slot, pl.ds(192, BLK), :]
            dof[rows, :] = do
            dot_[:, rows] = jnp.transpose(do.astype(jnp.float32))
        n_ch = s // (CH // (2 * SUP)) + 1

        def score(j, m8):
            for t in range(CH // SUP):
                r0 = pl.multiple_of(j * CH + t * SUP, SUP)
                st = mm(kr[pl.ds(r0, SUP), :], qt[...])
                st = jnp.where(diff <= ch * SUP - r0, st, NEG)
                s_buf[pl.ds(r0, SUP), :] = st
                m8 = jnp.maximum(m8, jnp.max(st.reshape(SUP // 8, 8, SUP), axis=0))
            return m8

        m8 = lax.fori_loop(0, n_ch, score, jnp.full((8, SUP), NEG, jnp.float32))
        m2 = jnp.max(m8, axis=0, keepdims=True) * c1
        ot[...] = jnp.zeros_like(ot)

        def forward(j, l8):
            base = pl.multiple_of(j * CH, CH)
            for t in range(CH // SUP):
                p = jnp.exp2(s_buf[pl.ds(base + t * SUP, SUP), :] * c1 - m2)
                l8 = l8 + jnp.sum(p.reshape(SUP // 8, 8, SUP), axis=0)
                p_buf[pl.ds(t * SUP, SUP), :] = p.astype(jnp.bfloat16)
            ot[...] += mm(vt[:, pl.ds(base, CH)], p_buf[...])
            return l8

        l8 = lax.fori_loop(0, n_ch, forward, jnp.zeros((8, SUP), jnp.float32))
        l = jnp.sum(l8, axis=0, keepdims=True)
        o = ot[...] / l
        lse2 = m2 + jnp.log2(l)
        delta = jnp.sum(o * dot_[...], axis=0, keepdims=True)
        o_rows = jnp.transpose(o)
        for i in range(2):
            od_send[2 * s + i, pl.ds(0, BLK), :] = o_rows[i * BLK:(i + 1) * BLK].astype(jnp.bfloat16)
        dqt[...] = jnp.zeros_like(dqt)

        def backward(j, carry):
            base = pl.multiple_of(j * CH, CH)
            for t in range(CH // SUP):
                rows = pl.ds(base + t * SUP, SUP)
                dp = mm(v[rows, :], dof[...], NT)
                p = jnp.exp2(s_buf[rows, :] * c1 - lse2)
                p_buf[pl.ds(t * SUP, SUP), :] = p.astype(jnp.bfloat16)
                ds_buf[pl.ds(t * SUP, SUP), :] = (p * (dp - delta) * scale).astype(jnp.bfloat16)
            for t in range(CH // SUP):
                rows = pl.ds(base + t * SUP, SUP)
                dkr[rows, :] += mm(ds_buf[pl.ds(t * SUP, SUP), :], qt[...], NT)
                dv[rows, :] += mm(p_buf[pl.ds(t * SUP, SUP), :], dof[...])
            dqt[...] += mm(kt[:, pl.ds(base, CH)], ds_buf[...])
            return carry

        lax.fori_loop(0, n_ch, backward, 0)
        for i in range(2):
            od_send[2 * s + i, pl.ds(BLK, 192), :] = dqt[:, pl.ds(i * BLK, BLK)].astype(jnp.bfloat16)
        for i in range(2):
            start(*od_copy(s, i))
        return carry

    lax.fori_loop(0, n_sup, superblock, 0)

    dwt[...] = jnp.zeros_like(dwt)

    def finish_keys(ch, carry):
        base = pl.multiple_of(ch * SUP, SUP)
        for q in range(2):
            rows = pl.ds(base + q * BLK, BLK)
            dkv_out[q, ch, pl.ds(0, BLK), :] = dkr[rows, pl.ds(0, 128)].astype(jnp.bfloat16)
            dkv_out[q, ch, pl.ds(BLK, BLK), :] = dv[rows, :].astype(jnp.bfloat16)
            dkv_out[q, ch, pl.ds(2 * BLK, 64), :] = pack_rope(dkr[rows, pl.ds(128, 128)][:, :64]).astype(jnp.bfloat16)
        dk_t = jnp.transpose(dkr[pl.ds(base, SUP), pl.ds(0, 128)])
        dv_t = jnp.transpose(dv[pl.ds(base, SUP), :])
        dkv_t = jnp.concatenate([dk_t, dv_t], axis=0).astype(jnp.bfloat16)
        dwt[...] += mm(dkv_t, latent_of(ch))
        return carry

    lax.fori_loop(0, n_chip, finish_keys, 0)
    pair_dkv = remote(dkv_out.at[1 - par], dkv_part, pair_sem.at[0], pair_sem.at[1], partner)
    pair_dkv.start()
    for q in range(2):
        dw_out[q] = jnp.transpose(dwt[pl.ds(q * 128, 128), :])
    pair_dw = remote(dw_out.at[1 - par], dw_part, pair_sem.at[2], pair_sem.at[3], partner)
    pair_dw.start()
    pair_dkv.wait()

    def add_pair(ch, carry):
        dkv_out[par, ch] = (dkv_out[par, ch].astype(jnp.float32) + dkv_part[ch].astype(jnp.float32)).astype(jnp.bfloat16)
        return carry

    lax.fori_loop(0, n_chip, add_pair, 0)
    pair_dw.wait()
    dw_all[par, chip] = dw_out[par] + dw_part[...]

    def dkv_copy(i):
        ch = lax.rem(chip + i, n_chip)
        return dkv_out.at[par, ch], dkv_recv.at[chip], dkv_ssem.at[i], dkv_rsem.at[chip], 2 * ch + par

    def deliver(h, carry):
        arrived(od_recv.at[h], od_rsem.at[h])
        o_out[h] = od_recv[h, pl.ds(0, BLK), :]
        dq_out[h] = od_recv[h, pl.ds(BLK, 192), :]
        return carry

    def send_dkv(step):
        per = -(-n_chip // nz)
        if step < nz:
            def go(i, carry):
                start(*dkv_copy(i))
                return carry

            lax.fori_loop(step * per, min((step + 1) * per, n_chip), go, 0)
        else:
            lax.fori_loop(0, n_chip, deliver, 0)

    def dw_copy(q, h):
        dst = dwk_out if q == 0 else dwv_out
        return pltpu.make_async_copy(dw_all.at[q, h], dst.at[:, h, 0], dw_sem.at[q, h])

    def put_dw(zq):
        for q in range(2):
            def go(i, carry):
                dw_copy(q, zq * 4 + i).start()
                return carry

            lax.fori_loop(0, 4, go, 0)

    finish_w = gather(dw_all, 512, True, wg_rz, wg_rp, wg_sz, wg_sx, wg_sp, send_dkv, put_dw)

    finish_c()
    finish_w()

    def drain(i, carry):
        sent(*q_copy(i))
        sent(*dkv_copy(i))
        sent(*od_copy(i // 2, i % 2))
        arrived(dkv_recv.at[i], dkv_rsem.at[i])
        for q in range(2):
            dw_copy(q, i).wait()
        return carry

    lax.fori_loop(0, n_chip, drain, 0)


def solution(mesh):
    n_dev = mesh.shape["cp"]
    n_chip = n_dev // 2
    nz = n_chip // (NX * NY)
    seq = n_dev * BLK
    seq_spec = P("cp")

    def local_step(queries, latent, key_rope, w_uk, w_uv, d_out):
        head = lax.axis_index("cp") // 2
        qd = jnp.concatenate([queries.transpose(1, 2, 0), d_out.transpose(1, 0, 2)], axis=1)
        cr = jnp.concatenate([latent[:, 128 * i:128 * (i + 1)] for i in range(4)] + [key_rope.T], axis=0)
        wk = lax.dynamic_index_in_dim(w_uk, head, 1, keepdims=False)
        wv = lax.dynamic_index_in_dim(w_uv, head, 1, keepdims=False)
        bf, f32 = jnp.bfloat16, jnp.float32
        vm = pl.BlockSpec(memory_space=pltpu.VMEM)
        dma = pltpu.SemaphoreType.DMA
        gather_sems = [dma((4, nz, 2)), dma((4, nz)), dma((max(2 * nz - 2, 2), nz)), dma((4, nz)), dma((4, nz))]
        o, dq, dkv, dwk, dwv = pl.pallas_call(
            functools.partial(kernel, nz, queries.shape[-1]),
            out_shape=(jax.ShapeDtypeStruct((n_chip, BLK, 128), bf),
                       jax.ShapeDtypeStruct((n_chip, 192, BLK), bf),
                       jax.ShapeDtypeStruct((n_chip, MSG, 128), bf),
                       jax.ShapeDtypeStruct((512, n_chip, 1, 128), f32),
                       jax.ShapeDtypeStruct((512, n_chip, 1, 128), f32)),
            in_specs=[vm] * 4,
            out_specs=(vm, vm, vm, pl.BlockSpec(memory_space=pl.ANY), pl.BlockSpec(memory_space=pl.ANY)),
            scratch_shapes=[
                pltpu.VMEM((n_chip, MSG, 128), bf),
                pltpu.VMEM((2, n_chip, 512, 128), f32),
                pltpu.VMEM((512, 256), bf),
                pltpu.VMEM((256, 512), bf),
                pltpu.VMEM((n_chip, MSG, 128), bf),
                pltpu.VMEM((2, n_chip, CMSG, 128), bf),
                pltpu.VMEM((seq, 256), bf),
                pltpu.VMEM((seq, 128), bf),
                pltpu.VMEM((192, seq), bf),
                pltpu.VMEM((128, seq), bf),
                pltpu.VMEM((seq, SUP), f32),
                pltpu.VMEM((CH, SUP), bf),
                pltpu.VMEM((CH, SUP), bf),
                pltpu.VMEM((seq, 256), f32),
                pltpu.VMEM((seq, 128), f32),
                pltpu.VMEM((256, SUP), bf),
                pltpu.VMEM((SUP, 128), bf),
                pltpu.VMEM((128, SUP), f32),
                pltpu.VMEM((128, SUP), f32),
                pltpu.VMEM((192, SUP), f32),
                pltpu.VMEM((n_chip, MSG, 128), bf),
                pltpu.VMEM((2, n_chip, MSG, 128), bf),
                pltpu.VMEM((n_chip, MSG, 128), bf),
                pltpu.VMEM((256, 512), f32),
                pltpu.VMEM((2, 512, 128), f32),
                pltpu.VMEM((512, 128), f32),
                dma((n_chip,)), dma((n_chip,)), dma((n_chip,)), dma((n_chip,)), dma((n_chip,)), dma((n_chip,)),
                dma((4,)), dma((2, n_chip)),
            ] + gather_sems + gather_sems,
            compiler_params=pltpu.CompilerParams(
                collective_id=0, has_side_effects=True, vmem_limit_bytes=60 * 1024 * 1024),
        )(qd, cr, wk, wv)
        attn_out = o.transpose(1, 0, 2)
        d_query = dq.transpose(2, 0, 1)
        d_latent = (jnp.einsum("htd,lhd->tl", dkv[:, :BLK], w_uk, preferred_element_type=f32)
                    + jnp.einsum("htd,lhd->tl", dkv[:, BLK:2 * BLK], w_uv, preferred_element_type=f32)).astype(bf)
        dr = jnp.sum(dkv[:, 2 * BLK:].astype(f32), axis=0)
        d_key_rope = jnp.concatenate([dr[:, :64], dr[:, 64:]], axis=0).astype(bf)
        return (attn_out, d_query, d_latent, d_key_rope,
                dwk.reshape(512, n_chip, 128), dwv.reshape(512, n_chip, 128))

    return jax.shard_map(local_step, mesh=mesh,
                         in_specs=(seq_spec, seq_spec, seq_spec, P(), P(), seq_spec),
                         out_specs=(seq_spec, seq_spec, seq_spec, seq_spec, P(), P()),
                         check_vma=False)
```

time: 199 us -> 193 us (0.970)
  the two profiles are of different devices: /device:TPU:5 before, /device:TPU:29 now
where the time goes in v2:
time: 193 us; the launch traced here: 192 us
  Pallas kernels  166 us (86%)
  local copies, waits for them, and re-layouts  17.6 us (9%)
  matrix products  4.72 us (2%)
  other arithmetic  3.3 us (2%)
    pallas_call x1, Pallas kernels, local_step(): pl.pallas_call(functools.partial(kernel, nz, queries.shape[-1]), out_shap...  166 us
    unnamed x26, local copies, waits for them, and re-layouts  16 us

profile of v2, /device:TPU:29, one launch (start us, length us, event | category | flops | bytes accessed | tf_op | source)
XLA Modules:
  0.0 192.4 jit_solution(17111946454570023852)
XLA Ops:
  0.6 0.0 copy-start.3
  0.7 0.9 slice_dynamic-update-slice_fusion.3
  1.6 0.8 slice_dynamic-update-slice_fusion.2
  2.3 0.8 slice_dynamic-update-slice_fusion.1
  3.1 0.8 slice_dynamic-update-slice_fusion
  3.9 0.7 bitcast_dynamic-update-slice_fusion.cr_ref
  4.6 1.2 copy.34
  5.8 2.3 %pad_maximum_fusion.qd_ref = bf16[16,320,128]{2,1,0:T(8,128)(2,1)} fusion(bf16[16,128,128]{2,1,0:T(8,128)(2,1)S(1)} %bitcast.24, bf16[16,192,128]{2,1,0:T(8,128)(2,1)} %bitcast.26), kind=kLoop, calls=%fused_computation | loop fusion | flops 2621440 | bytes 2621440 | tf_op jit(solution)/shard_map/concatenate | solution.py:442
  8.1 0.0 copy-done.3
  8.1 0.5 copy.23
  8.7 1.0 copy-done.2
  9.7 0.5 copy.24
  10.3 0.7 dynamic-slice_bitcast_fusion
  11.0 166.1 %shard_map.109 = (bf16[16,128,128]{2,1,0:T(8,128)(2,1)}, bf16[16,192,128]{2,1,0:T(8,128)(2,1)}, bf16[16,320,128]{2,1,0:T(8,128)(2,1)}, f32[512,16,1,128]{3,2,1,0:T(1,128)}, f32[512,16,1,128]{3,2,1,0:T(1,128)}) custom-call(bf16[16,320,128]{2,1,0:T(8,128)(2,1)} %pad_maximum_fusion.qd_ref, bf16[576,128]{1,0:T(8,128)(2,1)} %copy-done.6, ...), custom_call_target="tpu_custom_call" | custom-call | tf_op jit(solution)/shard_map/pallas_call | solution.py:450
  177.1 2.2 %copy.27 = bf16[128,16,128]{2,1,0:T(8,128)(2,1)} copy(bf16[128,16,128]{2,0,1:T(8,128)(2,1)} %bitcast.27) | data formatting | bytes 1048576
  179.2 1.0 slice_reduce_fusion
  180.2 0.1 fusion.6
  180.3 0.7 copy.28
  181.0 2.0 %convolution_bitcast_fusion = f32[128,512]{1,0:T(8,128)S(1)} fusion(bf16[16,320,128]{2,1,0:T(8,128)(2,1)} %get-tuple-element.13, bf16[512,16,128]{2,1,0:T(8,128)(2,1)S(1)} %copy-done.2), kind=kOutput, calls=%fused_computation.1 | convolution fusion | flops 268435456 | bytes 2883584 | tf_op jit(solution)/shard_map/htd,lhd->tl/dot_general | solution.py:495
  183.1 2.7 %fusion.1 = bf16[128,512]{1,0:T(8,128)(2,1)} fusion(f32[128,512]{1,0:T(8,128)S(1)} %convolution_bitcast_fusion, bf16[16,320,128]{2,1,0:T(8,128)(2,1)} %get-tuple-element.13, bf16[512,16,128]{2,1,0:T(8,128)(2,1)S(1)} %copy-done.4), kind=kOutput, calls=%fused_computation.4 | convolution fusion | flops 268566528 | bytes 3014656 | tf_op jit(solution)/shard_map/htd,lhd->tl/dot_general | solution.py:494
  185.8 0.9 copy.42
  186.7 2.1 %copy.43 = f32[512,16,128]{2,1,0:T(8,128)} copy(f32[512,16,128]{2,1,0:T(8,128)S(1)} %bitcast.23) | data formatting | bytes 8388608
  188.8 1.6 copy-done
  190.4 2.0 %copy.44 = f32[512,16,128]{2,1,0:T(8,128)} copy(f32[512,16,128]{2,1,0:T(8,128)S(1)} %bitcast.22) | data formatting | bytes 8388608
  (11 shorter events, 0.0 us)
Async XLA Ops:
  0.6 7.5 %copy-start.3 = (bf16[512,16,128]{2,1,0:T(8,128)(2,1)S(1)}, bf16[512,16,128]{2,1,0:T(8,128)(2,1)}, u32[]{:S(2)}) copy-start(bf16[512,16,128]{2,1,0:T(8,128)(2,1)} %param.9) | copy-start | bytes 6291460
  4.6 4.1 %copy-start.6 = (bf16[576,128]{1,0:T(8,128)(2,1)}, bf16[576,128]{1,0:T(8,128)(2,1)S(1)}, u32[]{:S(2)}) copy-start(bf16[576,128]{1,0:T(8,128)(2,1)S(1)} %bitcast_dynamic-update-slice_fusion.cr_ref) | copy-start | bytes 442372
  8.1 1.6 copy-start.2
  181.0 2.0 %copy-start.4 = (bf16[512,16,128]{2,1,0:T(8,128)(2,1)S(1)}, bf16[512,16,128]{2,1,0:T(8,128)(2,1)}, u32[]{:S(2)}) copy-start(bf16[512,16,128]{2,1,0:T(8,128)(2,1)} %param.9) | copy-start | bytes 6291460
  181.0 4.8 %copy-start.5 = (bf16[16,192,128]{2,1,0:T(8,128)(2,1)S(1)}, bf16[16,192,128]{2,1,0:T(8,128)(2,1)}, u32[]{:S(2)}) copy-start(bf16[16,192,128]{2,1,0:T(8,128)(2,1)} %get-tuple-element.12) | copy-start | bytes 2359300
  183.1 3.6 %copy-start.1 = (f32[512,16,1,128]{3,2,1,0:T(1,128)S(1)}, f32[512,16,1,128]{3,2,1,0:T(1,128)}, u32[]{:S(2)}) copy-start(f32[512,16,1,128]{3,2,1,0:T(1,128)} %get-tuple-element.14) | copy-start | bytes 12582916
  186.7 3.7 %copy-start = (f32[512,16,1,128]{3,2,1,0:T(1,128)S(1)}, f32[512,16,1,128]{3,2,1,0:T(1,128)}, u32[]{:S(2)}) copy-start(f32[512,16,1,128]{3,2,1,0:T(1,128)} %get-tuple-element.15) | copy-start | bytes 12582916
